TPU v7x, 128 devices: a whole 4x4x4 slice. The times are simulated.
128 devices in a mesh: seq: 16 (over x, y), head: 8 (over z, core).
Axes of the slice: x: 4, y: 4, z: 4, core: 2. Of those that a mesh axis runs over, the one named last changes fastest.
Arguments:
- queries: bfloat16 [4096, 12288], P('seq', 'head'), may hold values from -256 to 256
- own_latent: bfloat16 [4096, 576], P('seq'), may hold values from -16 to 16
- cache: bfloat16 [512, 128, 576], P('seq', 'head'), may hold values from -6 to 6
- block_list: int32 [16, 32], replicated, may hold values from 0 to 511, as said below
- offsets: int32 [16, 32], P('seq'), may hold values from -4096 to 4096
- tile_mask: int32 [16, 2, 32], P('seq'), may hold values 0 or 1
- w_uk: bfloat16 [64, 128, 512], P('head'), may hold values from -0.5 to 0.5
- w_uv: bfloat16 [64, 512, 128], P('head'), may hold values from -0.25 to 0.25
- w_o: bfloat16 [8192, 7168], P('head'), may hold values from -0.0625 to 0.0625
Outputs:
- layer_out: bfloat16 [4096, 7168], P('seq', 'head')
Inputs may be any that keep to these rules, and one draw needn't show every extreme that they name: `block_list`: entry (r, j) names a pooled span whose owner is index entry // 32 of seq. In each row no owner is named more than 4 times, and at least one owner is named exactly 4 times.
All inputs are finite; a program needn't handle non-finite values. No bound on the sum of `tile_mask` on one device may be relied on, other than what follows from the above.
Results may differ from a plain program's by a relative error of at most 0.015.
Values may be sent and summed in bfloat16 or wider, within the bound.
No kernel may reach another device: no remote copies, remote signals or barrier semaphores. Data moves between devices by JAX's collectives and lax.ppermute only.
A program may use at most 128 MiB of HBM per device.

v0:
```python
import jax
import jax.numpy as jnp
from jax import lax
from jax.sharding import PartitionSpec as P

MOST = 4
THETA = 50000.0


def rerotate(blocks, shift, latent_width):
    rotary_width = blocks.shape[-1] - latent_width
    halfway = rotary_width // 2
    inverse = THETA ** (-jnp.arange(halfway, dtype=jnp.float32) * 2.0 / rotary_width)
    angles = shift.astype(jnp.float32)[:, None] * inverse[None, :]
    cosine_table = jnp.cos(angles)[:, None, :]
    sine_table = jnp.sin(angles)[:, None, :]
    rotary = blocks[..., latent_width:].astype(jnp.float32)
    first_half = rotary[..., :halfway]
    second_half = rotary[..., halfway:]
    turned = jnp.concatenate(
        [
            first_half * cosine_table - second_half * sine_table,
            second_half * cosine_table + first_half * sine_table,
        ],
        axis=-1,
    )
    return jnp.concatenate([blocks[..., :latent_width], turned.astype(jnp.bfloat16)], axis=-1)


def allowed_keys(tiles, query_rows, block_rows):
    listed_mask = jnp.repeat(jnp.repeat(tiles > 0, block_rows, axis=0), block_rows, axis=1)
    causal = jnp.tril(jnp.ones((query_rows, query_rows), jnp.bool_))
    return jnp.concatenate([causal, listed_mask], axis=1)


def attend(grouped, context, allowed, key_maps, value_maps):
    nope_width = key_maps.shape[1]
    latent_width = key_maps.shape[2]
    factor = grouped.shape[-1] ** (-0.5)
    value_latent = context[:, :latent_width]

    def one_head(inputs):
        head_query, key_map, value_map = inputs
        query_latent = jnp.dot(
            head_query[:, :nope_width], key_map, preferred_element_type=jnp.float32
        ).astype(jnp.bfloat16)
        query_full = jnp.concatenate([query_latent, head_query[:, nope_width:]], axis=1)
        scores = (
            lax.dot_general(
                query_full, context, (((1,), (1,)), ((), ())), preferred_element_type=jnp.float32
            )
            * factor
        )
        scores = jnp.where(allowed, scores, -1e30)
        highest = jnp.max(scores, axis=1, keepdims=True)
        weights = jnp.exp(scores - highest)
        denominator = jnp.sum(weights, axis=1, keepdims=True)
        shares = (weights / denominator).astype(jnp.bfloat16)
        mixed_latent = jnp.dot(shares, value_latent, preferred_element_type=jnp.float32).astype(
            jnp.bfloat16
        )
        return jnp.dot(mixed_latent, value_map, preferred_element_type=jnp.float32).astype(
            jnp.bfloat16
        )

    per_head = lax.map(one_head, (jnp.transpose(grouped, (1, 0, 2)), key_maps, value_maps))
    return jnp.transpose(per_head, (1, 0, 2)).reshape(grouped.shape[0], -1)


def per_device(queries, own_latent, cache, block_list, offsets, tile_mask, w_uk, w_uv, w_o):
    seq_count = lax.axis_size("seq")
    seq_index = lax.axis_index("seq")
    spans_held = cache.shape[0]
    latent_full = cache.shape[2]
    listed_count = block_list.shape[1]
    owners = block_list // spans_held
    within = block_list % spans_held
    earlier = jnp.tril(jnp.ones((listed_count, listed_count), jnp.bool_), -1)
    same_owner = owners[:, :, None] == owners[:, None, :]
    ranking = jnp.sum(same_owner & earlier[None], axis=2)
    slot_ids = jnp.arange(MOST, dtype=jnp.int32)
    matches = (owners == seq_index)[:, :, None] & (ranking[:, :, None] == slot_ids[None, None, :])
    send_index = jnp.sum(jnp.where(matches, within[:, :, None], 0), axis=1)
    my_owners = lax.dynamic_index_in_dim(owners, seq_index, 0, keepdims=False)
    my_ranking = lax.dynamic_index_in_dim(ranking, seq_index, 0, keepdims=False)
    flat_slot = my_owners * MOST + my_ranking
    arrived = lax.all_to_all(cache[send_index], "seq", split_axis=0, concat_axis=0, tiled=True)
    picked = arrived.reshape(seq_count * MOST, cache.shape[1], latent_full)[flat_slot]
    blocks = lax.all_gather(picked, "head", axis=1, tiled=True)
    latent_width = w_uk.shape[2]
    block_rows = blocks.shape[1]
    turned = rerotate(blocks, offsets[0], latent_width).reshape(
        listed_count * block_rows, latent_full
    )
    context = jnp.concatenate([own_latent, turned], axis=0)
    query_rows = own_latent.shape[0]
    allowed = allowed_keys(tile_mask[0], query_rows, block_rows)
    head_width = w_uk.shape[1] + latent_full - latent_width
    grouped = queries.reshape(query_rows, -1, head_width)
    head_out = attend(grouped, context, allowed, w_uk, w_uv)
    partial_value = jnp.dot(head_out, w_o, preferred_element_type=jnp.float32)
    result = lax.psum_scatter(
        partial_value.astype(jnp.bfloat16), "head", scatter_dimension=1, tiled=True
    )
    return result


def solution(mesh):
    placed = (
        P("seq", "head"),
        P("seq", None),
        P("seq", "head", None),
        P(),
        P("seq", None),
        P("seq", None, None),
        P("head", None, None),
        P("head", None, None),
        P("head", None),
    )
    return jax.shard_map(
        per_device, mesh=mesh, in_specs=placed, out_specs=P("seq", "head"), check_vma=False
    )
```

profile of v0, /device:TPU:0, one launch (start us, length us, event | category | flops | bytes accessed | tf_op | source)
XLA Modules:
  0.0 265.0 jit_solution(6012045879321765092)
XLA Ops:
  6.6 0.8 add_select_fusion
  7.3 0.7 broadcast_compare_fusion
  8.1 0.5 convert_reduce_fusion
  9.0 1.8 gather_fusion
  10.7 7.3 %all-to-all-start = ((bf16[16,4,16,576]{3,2,1,0:T(8,128)(2,1)}), bf16[16,4,16,576]{3,2,1,0:T(8,128)(2,1)S(1)}, u32[]{:S(2)}, u32[]{:S(2)}) async-start(bf16[16,4,16,576]{3,2,1,0:T(8,128)(2,1)} %bitcast.7), calls=%async_computation | async-start | bytes 2621440 | tf_op jit(solution)/shard_map/all_to_all | solution.py:87
  18.1 20.7 %all-to-all-done = bf16[16,4,16,576]{3,2,1,0:T(8,128)(2,1)S(1)} async-done(((bf16[16,4,16,576]{3,2,1,0:T(8,128)(2,1)}), bf16[16,4,16,576]{3,2,1,0:T(8,128)(2,1)S(1)}, u32[]{:S(2)}, u32[]{:S(2)}) %all-to-all-start) | async-done | bytes 1179680 | tf_op jit(solution)/shard_map/all_to_all | solution.py:87
  38.8 1.5 gather_fusion.1
  40.4 0.2 copy.24
  40.6 2.1 broadcast_in_dim.33
  42.7 0.7 copy.34
  43.5 0.3 copy.22
  44.0 1.4 pad_add_fusion
  45.4 30.7 %all-gather.3.cloned.1.call-done = bf16[32,128,576]{2,1,0:T(8,128)(2,1)} async-done(((bf16[32,16,576]{2,1,0:T(8,128)(2,1)}), bf16[32,128,576]{2,1,0:T(8,128)(2,1)}) %all-gather.3.cloned.1.call-update) | async-done | bytes 4718608 | tf_op jit(solution)/shard_map/all_gather | solution.py:89
  76.0 1.5 slice_convert_fusion
  77.5 0.9 subtract_convert_fusion
  78.4 2.2 slice-done
  80.6 1.1 pad_maximum_fusion.1
  81.7 2.9 %pad_maximum_fusion = bf16[4352,576]{1,0:T(8,128)(2,1)} fusion(bf16[256,576]{1,0:T(8,128)(2,1)S(1)} %copy.24, bf16[4096,576]{1,0:T(8,128)(2,1)S(1)} %bitcast.53), kind=kLoop, calls=%fused_computation.28 | loop fusion | flops 10027008 | bytes 10027008 | tf_op jit(solution)/shard_map/concatenate | solution.py:95
  84.7 2.5 fusion.18
  87.1 115.0 %while.10 = (s32[]{:T(128)}, bf16[8,256,128]{1,2,0:T(8,128)(2,1)S(1)}, bf16[8,256,192]{1,2,0:T(8,128)(2,1)S(1)}, bf16[8,128,512]{2,1,0:T(8,128)(2,1)}, bf16[4352...) while((s32[]{:T(128)}, ...), condition=%wide.region_5.6_spmd, body=%wide.region_2.5_spmd.sunk | while | flops 2501213696 | bytes 43456640 | solution.py:66
  87.3 1.1 convolution_convert_fusion.3
  88.4 4.9 %fusion.41 = (f32[256]{0:T(256)S(1)}, f32[256,4352]{1,0:T(8,128)S(1)}) fusion(pred[256,4352]{1,0:T(32,128)(4,1)} %get-tuple-element.172, bf16[4352,576]{1,0:T(8,128)(2,1)} %get-tuple-element.171, bf16[256,64]{1,0:T(8,128)(2,1)S(1)} %slice.54, bf16[256,512]{1,0:T(8,128)(2,1)S(1)} %convolution_convert_fusion.3), kind=kOutput, calls=%fused_computation.63.clone.1 | convolution fusion | flops 1287388928 | bytes 10880000 | tf_op jit(solution)/shard_map/while/body/eval_jaxpr/dot_general | solution.py:49
  93.3 2.1 copy-done.2
  95.5 0.7 fusion.42
  96.2 5.1 %fusion.43 = bf16[1,256,128]{2,1,0:T(8,128)(2,1)S(1)} fusion(bf16[4352,512]{1,0:T(8,128)(2,1)} %get-tuple-element.173, f32[256,4352]{1,0:T(8,128)} %copy-done.2, f32[256]{0:T(256)S(1)} %fusion.42, f32[256]{0:T(256)S(1)} %get-tuple-element.148, bf16[8,512,128]{2,1,0:T(8,128)(2,1)} %get-tuple-element.174, s32[]{:T(128)} %get-tuple-element.158), kind=kOutput, calls=%fused_computation.12.clone.1 | convolution fusion | flops 1177911296 | bytes 9112064 | tf_op jit(solution)/shard_map/while/body/eval_jaxpr/dot_general | solution.py:62
  101.6 1.1 convolution_convert_fusion.3
  102.8 4.9 %fusion.41 = (f32[256]{0:T(256)S(1)}, f32[256,4352]{1,0:T(8,128)S(1)}) fusion(pred[256,4352]{1,0:T(32,128)(4,1)} %get-tuple-element.172, bf16[4352,576]{1,0:T(8,128)(2,1)} %get-tuple-element.171, bf16[256,64]{1,0:T(8,128)(2,1)S(1)} %slice.54, bf16[256,512]{1,0:T(8,128)(2,1)S(1)} %convolution_convert_fusion.3), kind=kOutput, calls=%fused_computation.63.clone.1 | convolution fusion | flops 1287388928 | bytes 10880000 | tf_op jit(solution)/shard_map/while/body/eval_jaxpr/dot_general | solution.py:49
  107.7 2.1 copy-done.2
  109.9 0.7 fusion.42
  110.6 5.1 %fusion.43 = bf16[1,256,128]{2,1,0:T(8,128)(2,1)S(1)} fusion(bf16[4352,512]{1,0:T(8,128)(2,1)} %get-tuple-element.173, f32[256,4352]{1,0:T(8,128)} %copy-done.2, f32[256]{0:T(256)S(1)} %fusion.42, f32[256]{0:T(256)S(1)} %get-tuple-element.148, bf16[8,512,128]{2,1,0:T(8,128)(2,1)} %get-tuple-element.174, s32[]{:T(128)} %get-tuple-element.158), kind=kOutput, calls=%fused_computation.12.clone.1 | convolution fusion | flops 1177911296 | bytes 9112064 | tf_op jit(solution)/shard_map/while/body/eval_jaxpr/dot_general | solution.py:62
  116.0 1.1 convolution_convert_fusion.3
  117.2 4.9 %fusion.41 = (f32[256]{0:T(256)S(1)}, f32[256,4352]{1,0:T(8,128)S(1)}) fusion(pred[256,4352]{1,0:T(32,128)(4,1)} %get-tuple-element.172, bf16[4352,576]{1,0:T(8,128)(2,1)} %get-tuple-element.171, bf16[256,64]{1,0:T(8,128)(2,1)S(1)} %slice.54, bf16[256,512]{1,0:T(8,128)(2,1)S(1)} %convolution_convert_fusion.3), kind=kOutput, calls=%fused_computation.63.clone.1 | convolution fusion | flops 1287388928 | bytes 10880000 | tf_op jit(solution)/shard_map/while/body/eval_jaxpr/dot_general | solution.py:49
  122.1 2.1 copy-done.2
  124.2 0.7 fusion.42
  125.0 5.1 %fusion.43 = bf16[1,256,128]{2,1,0:T(8,128)(2,1)S(1)} fusion(bf16[4352,512]{1,0:T(8,128)(2,1)} %get-tuple-element.173, f32[256,4352]{1,0:T(8,128)} %copy-done.2, f32[256]{0:T(256)S(1)} %fusion.42, f32[256]{0:T(256)S(1)} %get-tuple-element.148, bf16[8,512,128]{2,1,0:T(8,128)(2,1)} %get-tuple-element.174, s32[]{:T(128)} %get-tuple-element.158), kind=kOutput, calls=%fused_computation.12.clone.1 | convolution fusion | flops 1177911296 | bytes 9112064 | tf_op jit(solution)/shard_map/while/body/eval_jaxpr/dot_general | solution.py:62
  130.4 1.1 convolution_convert_fusion.3
  131.5 4.9 %fusion.41 = (f32[256]{0:T(256)S(1)}, f32[256,4352]{1,0:T(8,128)S(1)}) fusion(pred[256,4352]{1,0:T(32,128)(4,1)} %get-tuple-element.172, bf16[4352,576]{1,0:T(8,128)(2,1)} %get-tuple-element.171, bf16[256,64]{1,0:T(8,128)(2,1)S(1)} %slice.54, bf16[256,512]{1,0:T(8,128)(2,1)S(1)} %convolution_convert_fusion.3), kind=kOutput, calls=%fused_computation.63.clone.1 | convolution fusion | flops 1287388928 | bytes 10880000 | tf_op jit(solution)/shard_map/while/body/eval_jaxpr/dot_general | solution.py:49
  136.5 2.1 copy-done.2
  138.6 0.7 fusion.42
  139.4 5.1 %fusion.43 = bf16[1,256,128]{2,1,0:T(8,128)(2,1)S(1)} fusion(bf16[4352,512]{1,0:T(8,128)(2,1)} %get-tuple-element.173, f32[256,4352]{1,0:T(8,128)} %copy-done.2, f32[256]{0:T(256)S(1)} %fusion.42, f32[256]{0:T(256)S(1)} %get-tuple-element.148, bf16[8,512,128]{2,1,0:T(8,128)(2,1)} %get-tuple-element.174, s32[]{:T(128)} %get-tuple-element.158), kind=kOutput, calls=%fused_computation.12.clone.1 | convolution fusion | flops 1177911296 | bytes 9112064 | tf_op jit(solution)/shard_map/while/body/eval_jaxpr/dot_general | solution.py:62
  144.8 1.1 convolution_convert_fusion.3
  145.9 4.9 %fusion.41 = (f32[256]{0:T(256)S(1)}, f32[256,4352]{1,0:T(8,128)S(1)}) fusion(pred[256,4352]{1,0:T(32,128)(4,1)} %get-tuple-element.172, bf16[4352,576]{1,0:T(8,128)(2,1)} %get-tuple-element.171, bf16[256,64]{1,0:T(8,128)(2,1)S(1)} %slice.54, bf16[256,512]{1,0:T(8,128)(2,1)S(1)} %convolution_convert_fusion.3), kind=kOutput, calls=%fused_computation.63.clone.1 | convolution fusion | flops 1287388928 | bytes 10880000 | tf_op jit(solution)/shard_map/while/body/eval_jaxpr/dot_general | solution.py:49
  150.9 2.1 copy-done.2
  153.0 0.7 fusion.42
  153.7 5.1 %fusion.43 = bf16[1,256,128]{2,1,0:T(8,128)(2,1)S(1)} fusion(bf16[4352,512]{1,0:T(8,128)(2,1)} %get-tuple-element.173, f32[256,4352]{1,0:T(8,128)} %copy-done.2, f32[256]{0:T(256)S(1)} %fusion.42, f32[256]{0:T(256)S(1)} %get-tuple-element.148, bf16[8,512,128]{2,1,0:T(8,128)(2,1)} %get-tuple-element.174, s32[]{:T(128)} %get-tuple-element.158), kind=kOutput, calls=%fused_computation.12.clone.1 | convolution fusion | flops 1177911296 | bytes 9112064 | tf_op jit(solution)/shard_map/while/body/eval_jaxpr/dot_general | solution.py:62
  159.2 1.1 convolution_convert_fusion.3
  160.3 4.9 %fusion.41 = (f32[256]{0:T(256)S(1)}, f32[256,4352]{1,0:T(8,128)S(1)}) fusion(pred[256,4352]{1,0:T(32,128)(4,1)} %get-tuple-element.172, bf16[4352,576]{1,0:T(8,128)(2,1)} %get-tuple-element.171, bf16[256,64]{1,0:T(8,128)(2,1)S(1)} %slice.54, bf16[256,512]{1,0:T(8,128)(2,1)S(1)} %convolution_convert_fusion.3), kind=kOutput, calls=%fused_computation.63.clone.1 | convolution fusion | flops 1287388928 | bytes 10880000 | tf_op jit(solution)/shard_map/while/body/eval_jaxpr/dot_general | solution.py:49
  165.3 2.1 copy-done.2
  167.4 0.7 fusion.42
  168.1 5.1 %fusion.43 = bf16[1,256,128]{2,1,0:T(8,128)(2,1)S(1)} fusion(bf16[4352,512]{1,0:T(8,128)(2,1)} %get-tuple-element.173, f32[256,4352]{1,0:T(8,128)} %copy-done.2, f32[256]{0:T(256)S(1)} %fusion.42, f32[256]{0:T(256)S(1)} %get-tuple-element.148, bf16[8,512,128]{2,1,0:T(8,128)(2,1)} %get-tuple-element.174, s32[]{:T(128)} %get-tuple-element.158), kind=kOutput, calls=%fused_computation.12.clone.1 | convolution fusion | flops 1177911296 | bytes 9112064 | tf_op jit(solution)/shard_map/while/body/eval_jaxpr/dot_general | solution.py:62
  173.6 1.1 convolution_convert_fusion.3
  174.7 4.9 %fusion.41 = (f32[256]{0:T(256)S(1)}, f32[256,4352]{1,0:T(8,128)S(1)}) fusion(pred[256,4352]{1,0:T(32,128)(4,1)} %get-tuple-element.172, bf16[4352,576]{1,0:T(8,128)(2,1)} %get-tuple-element.171, bf16[256,64]{1,0:T(8,128)(2,1)S(1)} %slice.54, bf16[256,512]{1,0:T(8,128)(2,1)S(1)} %convolution_convert_fusion.3), kind=kOutput, calls=%fused_computation.63.clone.1 | convolution fusion | flops 1287388928 | bytes 10880000 | tf_op jit(solution)/shard_map/while/body/eval_jaxpr/dot_general | solution.py:49
  179.6 2.1 copy-done.2
  181.8 0.7 fusion.42
  182.5 5.1 %fusion.43 = bf16[1,256,128]{2,1,0:T(8,128)(2,1)S(1)} fusion(bf16[4352,512]{1,0:T(8,128)(2,1)} %get-tuple-element.173, f32[256,4352]{1,0:T(8,128)} %copy-done.2, f32[256]{0:T(256)S(1)} %fusion.42, f32[256]{0:T(256)S(1)} %get-tuple-element.148, bf16[8,512,128]{2,1,0:T(8,128)(2,1)} %get-tuple-element.174, s32[]{:T(128)} %get-tuple-element.158), kind=kOutput, calls=%fused_computation.12.clone.1 | convolution fusion | flops 1177911296 | bytes 9112064 | tf_op jit(solution)/shard_map/while/body/eval_jaxpr/dot_general | solution.py:62
  187.9 1.1 convolution_convert_fusion.3
  189.1 4.9 %fusion.41 = (f32[256]{0:T(256)S(1)}, f32[256,4352]{1,0:T(8,128)S(1)}) fusion(pred[256,4352]{1,0:T(32,128)(4,1)} %get-tuple-element.172, bf16[4352,576]{1,0:T(8,128)(2,1)} %get-tuple-element.171, bf16[256,64]{1,0:T(8,128)(2,1)S(1)} %slice.54, bf16[256,512]{1,0:T(8,128)(2,1)S(1)} %convolution_convert_fusion.3), kind=kOutput, calls=%fused_computation.63.clone.1 | convolution fusion | flops 1287388928 | bytes 10880000 | tf_op jit(solution)/shard_map/while/body/eval_jaxpr/dot_general | solution.py:49
  194.0 2.1 copy-done.2
  196.1 0.7 fusion.42
  196.9 5.1 %fusion.43 = bf16[1,256,128]{2,1,0:T(8,128)(2,1)S(1)} fusion(bf16[4352,512]{1,0:T(8,128)(2,1)} %get-tuple-element.173, f32[256,4352]{1,0:T(8,128)} %copy-done.2, f32[256]{0:T(256)S(1)} %fusion.42, f32[256]{0:T(256)S(1)} %get-tuple-element.148, bf16[8,512,128]{2,1,0:T(8,128)(2,1)} %get-tuple-element.174, s32[]{:T(128)} %get-tuple-element.158), kind=kOutput, calls=%fused_computation.12.clone.1 | convolution fusion | flops 1177911296 | bytes 9112064 | tf_op jit(solution)/shard_map/while/body/eval_jaxpr/dot_general | solution.py:62
  202.2 10.9 %convolution_convert_fusion.1 = bf16[256,7168]{1,0:T(8,128)(2,1)} fusion(bf16[256,1024]{0,1:T(8,128)(2,1)S(1)} %bitcast.62, bf16[1024,7168]{1,0:T(8,128)(2,1)} %param.19), kind=kOutput, calls=%fused_computation.26 | convolution fusion | flops 3759931392 | bytes 18874368 | tf_op jit(solution)/shard_map/dot_general | solution.py:101
  213.1 5.9 %copy.27 = bf16[256,7168]{0,1:T(8,128)(2,1)} copy(bf16[256,7168]{1,0:T(8,128)(2,1)} %convolution_convert_fusion.1) | data formatting | bytes 7340032
  219.0 37.2 %reduce-scatter.4.cloned.1.call-done = bf16[896,256]{1,0:T(8,128)(2,1)} async-done(((bf16[7168,256]{1,0:T(8,128)(2,1)}), bf16[896,256]{1,0:T(8,128)(2,1)}) %reduce-scatter.4.cloned.1.call-update) | async-done | bytes 458768
  256.2 2.0 copy.28
  (83 shorter events, 2.7 us)
Async XLA Ops:
  6.5 2.4 copy-start
  6.5 33.9 %copy-start.5 = (bf16[256,576]{0,1:T(8,128)(2,1)S(1)}, bf16[256,576]{0,1:T(8,128)(2,1)}, u32[]{:S(2)}) copy-start(bf16[256,576]{0,1:T(8,128)(2,1)} %param.12) | copy-start | bytes 884740
  6.5 34.1 %copy-start.6 = (s32[1,2,32]{2,1,0:T(2,128)S(1)}, s32[1,2,32]{2,1,0:T(2,128)}, u32[]{:S(2)}) copy-start(s32[1,2,32]{2,1,0:T(2,128)} %param.16) | copy-start | bytes 772
  10.7 32.7 %copy-start.3 = (bf16[256,1536]{1,0:T(8,128)(2,1)S(1)}, bf16[256,1536]{1,0:T(8,128)(2,1)}, u32[]{:S(2)}) copy-start(bf16[256,1536]{1,0:T(8,128)(2,1)} %param.11) | copy-start | bytes 2359300
  10.7 33.1 %copy-start.7 = (s32[1,32]{1,0:T(1,128)S(1)}, s32[1,32]{1,0:T(1,128)}, u32[]{:S(2)}) copy-start(s32[1,32]{1,0:T(1,128)} %param.15) | copy-start | bytes 388
  10.7 28.1 %all-to-all-start = ((bf16[16,4,16,576]{3,2,1,0:T(8,128)(2,1)}), bf16[16,4,16,576]{3,2,1,0:T(8,128)(2,1)S(1)}, u32[]{:S(2)}, u32[]{:S(2)}) async-start(bf16[16,4,16,576]{3,2,1,0:T(8,128)(2,1)} %bitcast.7), calls=%async_computation | async-start | bytes 2621440 | tf_op jit(solution)/shard_map/all_to_all | solution.py:87
  18.0 58.0 %all-gather.3.cloned.1.call-start = ((), (), s32[]{:S(2)}) async-start(), calls=%async_computation.2 | async-start | bytes 5898240 | tf_op jit(solution)/shard_map/all_gather | solution.py:89
  40.3 215.9 %reduce-scatter.4.cloned.1.call-start = ((), (), s32[]{:S(2)}) async-start(), calls=%async_computation.3 | async-start | bytes 4128768
  78.4 2.2 slice-start
  84.7 2.5 copy-start.4
  93.3 2.1 copy-start.2
  107.7 2.1 copy-start.2
  122.1 2.1 copy-start.2
  136.5 2.1 copy-start.2
  150.9 2.1 copy-start.2
  165.2 2.1 copy-start.2
  179.6 2.1 copy-start.2
  194.0 2.1 copy-start.2
  202.2 56.0 %copy-start.1 = (bf16[32,16,576]{2,1,0:T(8,128)(2,1)S(1)}, bf16[32,16,576]{2,1,0:T(8,128)(2,1)}, u32[]{:S(2)}) copy-start(bf16[32,16,576]{2,1,0:T(8,128)(2,1)} %param.13) | copy-start | bytes 1769476
Sparse Core Ops, SparseCore 0:
  40.5 35.5 all-gather.2
  219.1 37.0 reduce-scatter.3
where the time goes:
time: 266 us; the launch traced here: 265 us
  matrix products  100 us (38%)
  waiting for transfers between devices  88.6 us (33%)
  local copies, waits for them, and re-layouts  35.9 us (13%)
  other arithmetic  18.6 us (7%)
  between operations  13.6 us (5%)
  starting transfers between devices  7.36 us (3%)
    dot_general x8, matrix products, one_head(): jnp.dot(mixed_latent, value_map, preferred_element_type=jnp.float32)  41.1 us
    dot_general x8, matrix products, one_head(): lax.dot_general(query_full, context, (((1,), (1,)), ((), ())), preferred_...  39.5 us
    unnamed x3, waiting for transfers between devices  37.2 us
    all_gather x1, waiting for transfers between devices, per_device(): blocks = lax.all_gather(picked, 'head', axis=1, tiled=True)  30.7 us
    all_to_all x1, waiting for transfers between devices, per_device(): lax.all_to_all(cache[send_index], 'seq', split_axis=0, concat_axis=0, til...  20.7 us
    while x16, local copies, waits for them, and re-layouts  17.1 us
    dot_general x1, matrix products, per_device(): partial_value = jnp.dot(head_out, w_o, preferred_element_type=jnp.float32)  10.9 us
    unnamed x19, local copies, waits for them, and re-layouts  9.16 us
  transfers between devices with their start and end apart: 3, of which 3 were waited for; matrix products, arithmetic and copies ran while one was open for 2% of the time, Pallas kernels for 0%

commit v1 on v0

--- a/solution.py
+++ b/solution.py
@@ -86,7 +86,8 @@
     flat_slot = my_owners * MOST + my_ranking
     arrived = lax.all_to_all(cache[send_index], "seq", split_axis=0, concat_axis=0, tiled=True)
     picked = arrived.reshape(seq_count * MOST, cache.shape[1], latent_full)[flat_slot]
-    blocks = lax.all_gather(picked, "head", axis=1, tiled=True)
+    sent = jnp.stack([picked] * lax.axis_size("head"))
+    blocks = jnp.concatenate(lax.all_to_all(sent, "head", 0, 0), axis=1)
     latent_width = w_uk.shape[2]
     block_rows = blocks.shape[1]
     turned = rerotate(blocks, offsets[0], latent_width).reshape(

time: 266 us -> 295 us (1.11)
  waiting for transfers between devices: 88.6 us -> 110 us
  starting transfers between devices: 7.36 us -> 12.6 us
  local copies, waits for them, and re-layouts: 35.9 us -> 39.3 us
    all_to_all x0 -> x1, waiting for transfers between devices: none -> 56 us  [per_device(): blocks = jnp.concatenate(lax.all_to_all(sent, 'head', 0, 0), axis=1)]
    all_gather x1 -> x0, waiting for transfers between devices: 30.7 us -> none  [per_device(): blocks = lax.all_gather(picked, 'head', axis=1, tiled=True)]
    all_to_all x0 -> x1, starting transfers between devices: none -> 5.45 us  [per_device(): blocks = jnp.concatenate(lax.all_to_all(sent, 'head', 0, 0), axis=1)]
    unnamed x3 -> x2, waiting for transfers between devices: 37.2 us -> 33.4 us
    reshape x0 -> x1, local copies, waits for them, and re-layouts: none -> 3.29 us  [per_device(): blocks = jnp.concatenate(lax.all_to_all(sent, 'head', 0, 0), axis=1)]
where the time goes in v1:
time: 295 us; the launch traced here: 294 us
  waiting for transfers between devices  110 us (37%)
  matrix products  101 us (34%)
  local copies, waits for them, and re-layouts  39.3 us (13%)
  other arithmetic  17.4 us (6%)
  between operations  13.6 us (5%)
  starting transfers between devices  12.6 us (4%)
    all_to_all x1, waiting for transfers between devices, per_device(): blocks = jnp.concatenate(lax.all_to_all(sent, 'head', 0, 0), axis=1)  56 us
    dot_general x8, matrix products, one_head(): jnp.dot(mixed_latent, value_map, preferred_element_type=jnp.float32)  41.1 us
    dot_general x8, matrix products, one_head(): lax.dot_general(query_full, context, (((1,), (1,)), ((), ())), preferred_...  39.5 us
    unnamed x2, waiting for transfers between devices  33.4 us
    all_to_all x1, waiting for transfers between devices, per_device(): lax.all_to_all(cache[send_index], 'seq', split_axis=0, concat_axis=0, til...  20.8 us
    while x16, local copies, waits for them, and re-layouts  17.1 us
    dot_general x1, matrix products, per_device(): partial_value = jnp.dot(head_out, w_o, preferred_element_type=jnp.float32)  11 us
    unnamed x19, local copies, waits for them, and re-layouts  9.15 us
  transfers between devices with their start and end apart: 3, of which 3 were waited for; matrix products, arithmetic and copies ran while one was open for 2% of the time, Pallas kernels for 0%

profile of v1, /device:TPU:0, one launch (start us, length us, event | category | flops | bytes accessed | tf_op | source)
XLA Modules:
  0.0 294.2 jit_solution(3870206598032400949)
XLA Ops:
  6.5 0.8 add_select_fusion
  7.3 0.7 broadcast_compare_fusion
  8.1 0.5 convert_reduce_fusion
  8.9 1.8 gather_fusion
  10.7 7.1 %all-to-all-start = ((bf16[16,4,16,576]{3,2,1,0:T(8,128)(2,1)}), bf16[16,4,16,576]{3,2,1,0:T(8,128)(2,1)S(1)}, u32[]{:S(2)}, u32[]{:S(2)}) async-start(bf16[16,4,16,576]{3,2,1,0:T(8,128)(2,1)} %bitcast.7), calls=%async_computation | async-start | bytes 2621440 | tf_op jit(solution)/shard_map/all_to_all | solution.py:87
  17.9 20.8 %all-to-all-done = bf16[16,4,16,576]{3,2,1,0:T(8,128)(2,1)S(1)} async-done(((bf16[16,4,16,576]{3,2,1,0:T(8,128)(2,1)}), bf16[16,4,16,576]{3,2,1,0:T(8,128)(2,1)S(1)}, u32[]{:S(2)}, u32[]{:S(2)}) %all-to-all-start) | async-done | bytes 1179680 | tf_op jit(solution)/shard_map/all_to_all | solution.py:87
  38.6 0.7 gather_fusion.1
  39.3 2.8 stack.2
  42.1 5.4 %all-to-all-start.1 = ((bf16[8,32,16,576]{3,2,1,0:T(8,128)(2,1)}), bf16[8,32,16,576]{3,2,1,0:T(8,128)(2,1)}, u32[]{:S(2)}, u32[]{:S(2)}) async-start(bf16[8,32,16,576]{3,2,1,0:T(8,128)(2,1)} %stack.2), calls=%async_computation.1 | async-start | bytes 10485760 | tf_op jit(solution)/shard_map/all_to_all | solution.py:90
  47.8 2.1 broadcast_in_dim.33
  49.9 0.7 copy.41
  51.2 1.4 pad_add_fusion
  52.5 56.0 %all-to-all-done.1 = bf16[8,32,16,576]{3,2,1,0:T(8,128)(2,1)} async-done(((bf16[8,32,16,576]{3,2,1,0:T(8,128)(2,1)}), bf16[8,32,16,576]{3,2,1,0:T(8,128)(2,1)}, u32[]{:S(2)}, u32[]{:S(2)}) %all-to-all-start.1) | async-done | bytes 4718624 | tf_op jit(solution)/shard_map/all_to_all | solution.py:90
  108.5 3.3 %copy.30 = bf16[32,8,16,576]{3,2,1,0:T(8,128)(2,1)S(1)} copy(bf16[32,8,16,576]{3,2,0,1:T(8,128)(2,1)} %bitcast.11) | data formatting | bytes 9437184 | tf_op jit(solution)/shard_map/reshape | solution.py:90
  112.1 0.4 slice.32
  112.5 0.9 subtract_convert_fusion
  113.4 1.1 pad_maximum_fusion.1
  114.5 3.0 %pad_maximum_fusion = bf16[4352,576]{1,0:T(8,128)(2,1)} fusion(bf16[256,576]{1,0:T(8,128)(2,1)S(1)} %copy.31, bf16[4096,576]{1,0:T(8,128)(2,1)S(1)} %bitcast.55), kind=kLoop, calls=%fused_computation.28 | loop fusion | flops 10027008 | bytes 10027008 | tf_op jit(solution)/shard_map/concatenate | solution.py:96
  117.5 2.5 fusion.18
  120.0 115.0 %while.10 = (s32[]{:T(128)}, bf16[8,256,128]{1,2,0:T(8,128)(2,1)S(1)}, bf16[8,256,192]{1,2,0:T(8,128)(2,1)S(1)}, bf16[8,128,512]{2,1,0:T(8,128)(2,1)}, bf16[4352...) while((s32[]{:T(128)}, ...), condition=%wide.region_5.6_spmd, body=%wide.region_2.5_spmd.sunk | while | flops 2501213696 | bytes 43456640 | solution.py:66
  120.1 1.1 convolution_convert_fusion.3
  121.2 4.9 %fusion.41 = (f32[256]{0:T(256)S(1)}, f32[256,4352]{1,0:T(8,128)S(1)}) fusion(pred[256,4352]{1,0:T(32,128)(4,1)} %get-tuple-element.180, bf16[4352,576]{1,0:T(8,128)(2,1)} %get-tuple-element.179, bf16[256,64]{1,0:T(8,128)(2,1)S(1)} %slice.54, bf16[256,512]{1,0:T(8,128)(2,1)S(1)} %convolution_convert_fusion.3), kind=kOutput, calls=%fused_computation.63.clone.1 | convolution fusion | flops 1287388928 | bytes 10880000 | tf_op jit(solution)/shard_map/while/body/eval_jaxpr/dot_general | solution.py:49
  126.2 2.1 copy-done.2
  128.3 0.7 fusion.42
  129.0 5.1 %fusion.43 = bf16[1,256,128]{2,1,0:T(8,128)(2,1)S(1)} fusion(bf16[4352,512]{1,0:T(8,128)(2,1)} %get-tuple-element.181, f32[256,4352]{1,0:T(8,128)} %copy-done.2, f32[256]{0:T(256)S(1)} %fusion.42, f32[256]{0:T(256)S(1)} %get-tuple-element.156, bf16[8,512,128]{2,1,0:T(8,128)(2,1)} %get-tuple-element.182, s32[]{:T(128)} %get-tuple-element.166), kind=kOutput, calls=%fused_computation.12.clone.1 | convolution fusion | flops 1177911296 | bytes 9112064 | tf_op jit(solution)/shard_map/while/body/eval_jaxpr/dot_general | solution.py:62
  134.5 1.1 convolution_convert_fusion.3
  135.6 4.9 %fusion.41 = (f32[256]{0:T(256)S(1)}, f32[256,4352]{1,0:T(8,128)S(1)}) fusion(pred[256,4352]{1,0:T(32,128)(4,1)} %get-tuple-element.180, bf16[4352,576]{1,0:T(8,128)(2,1)} %get-tuple-element.179, bf16[256,64]{1,0:T(8,128)(2,1)S(1)} %slice.54, bf16[256,512]{1,0:T(8,128)(2,1)S(1)} %convolution_convert_fusion.3), kind=kOutput, calls=%fused_computation.63.clone.1 | convolution fusion | flops 1287388928 | bytes 10880000 | tf_op jit(solution)/shard_map/while/body/eval_jaxpr/dot_general | solution.py:49
  140.5 2.1 copy-done.2
  142.7 0.7 fusion.42
  143.4 5.1 %fusion.43 = bf16[1,256,128]{2,1,0:T(8,128)(2,1)S(1)} fusion(bf16[4352,512]{1,0:T(8,128)(2,1)} %get-tuple-element.181, f32[256,4352]{1,0:T(8,128)} %copy-done.2, f32[256]{0:T(256)S(1)} %fusion.42, f32[256]{0:T(256)S(1)} %get-tuple-element.156, bf16[8,512,128]{2,1,0:T(8,128)(2,1)} %get-tuple-element.182, s32[]{:T(128)} %get-tuple-element.166), kind=kOutput, calls=%fused_computation.12.clone.1 | convolution fusion | flops 1177911296 | bytes 9112064 | tf_op jit(solution)/shard_map/while/body/eval_jaxpr/dot_general | solution.py:62
  148.8 1.1 convolution_convert_fusion.3
  150.0 4.9 %fusion.41 = (f32[256]{0:T(256)S(1)}, f32[256,4352]{1,0:T(8,128)S(1)}) fusion(pred[256,4352]{1,0:T(32,128)(4,1)} %get-tuple-element.180, bf16[4352,576]{1,0:T(8,128)(2,1)} %get-tuple-element.179, bf16[256,64]{1,0:T(8,128)(2,1)S(1)} %slice.54, bf16[256,512]{1,0:T(8,128)(2,1)S(1)} %convolution_convert_fusion.3), kind=kOutput, calls=%fused_computation.63.clone.1 | convolution fusion | flops 1287388928 | bytes 10880000 | tf_op jit(solution)/shard_map/while/body/eval_jaxpr/dot_general | solution.py:49
  154.9 2.1 copy-done.2
  157.1 0.7 fusion.42
  157.8 5.1 %fusion.43 = bf16[1,256,128]{2,1,0:T(8,128)(2,1)S(1)} fusion(bf16[4352,512]{1,0:T(8,128)(2,1)} %get-tuple-element.181, f32[256,4352]{1,0:T(8,128)} %copy-done.2, f32[256]{0:T(256)S(1)} %fusion.42, f32[256]{0:T(256)S(1)} %get-tuple-element.156, bf16[8,512,128]{2,1,0:T(8,128)(2,1)} %get-tuple-element.182, s32[]{:T(128)} %get-tuple-element.166), kind=kOutput, calls=%fused_computation.12.clone.1 | convolution fusion | flops 1177911296 | bytes 9112064 | tf_op jit(solution)/shard_map/while/body/eval_jaxpr/dot_general | solution.py:62
  163.2 1.1 convolution_convert_fusion.3
  164.4 4.9 %fusion.41 = (f32[256]{0:T(256)S(1)}, f32[256,4352]{1,0:T(8,128)S(1)}) fusion(pred[256,4352]{1,0:T(32,128)(4,1)} %get-tuple-element.180, bf16[4352,576]{1,0:T(8,128)(2,1)} %get-tuple-element.179, bf16[256,64]{1,0:T(8,128)(2,1)S(1)} %slice.54, bf16[256,512]{1,0:T(8,128)(2,1)S(1)} %convolution_convert_fusion.3), kind=kOutput, calls=%fused_computation.63.clone.1 | convolution fusion | flops 1287388928 | bytes 10880000 | tf_op jit(solution)/shard_map/while/body/eval_jaxpr/dot_general | solution.py:49
  169.3 2.1 copy-done.2
  171.4 0.7 fusion.42
  172.2 5.1 %fusion.43 = bf16[1,256,128]{2,1,0:T(8,128)(2,1)S(1)} fusion(bf16[4352,512]{1,0:T(8,128)(2,1)} %get-tuple-element.181, f32[256,4352]{1,0:T(8,128)} %copy-done.2, f32[256]{0:T(256)S(1)} %fusion.42, f32[256]{0:T(256)S(1)} %get-tuple-element.156, bf16[8,512,128]{2,1,0:T(8,128)(2,1)} %get-tuple-element.182, s32[]{:T(128)} %get-tuple-element.166), kind=kOutput, calls=%fused_computation.12.clone.1 | convolution fusion | flops 1177911296 | bytes 9112064 | tf_op jit(solution)/shard_map/while/body/eval_jaxpr/dot_general | solution.py:62
  177.6 1.1 convolution_convert_fusion.3
  178.7 4.9 %fusion.41 = (f32[256]{0:T(256)S(1)}, f32[256,4352]{1,0:T(8,128)S(1)}) fusion(pred[256,4352]{1,0:T(32,128)(4,1)} %get-tuple-element.180, bf16[4352,576]{1,0:T(8,128)(2,1)} %get-tuple-element.179, bf16[256,64]{1,0:T(8,128)(2,1)S(1)} %slice.54, bf16[256,512]{1,0:T(8,128)(2,1)S(1)} %convolution_convert_fusion.3), kind=kOutput, calls=%fused_computation.63.clone.1 | convolution fusion | flops 1287388928 | bytes 10880000 | tf_op jit(solution)/shard_map/while/body/eval_jaxpr/dot_general | solution.py:49
  183.7 2.1 copy-done.2
  185.8 0.7 fusion.42
  186.6 5.1 %fusion.43 = bf16[1,256,128]{2,1,0:T(8,128)(2,1)S(1)} fusion(bf16[4352,512]{1,0:T(8,128)(2,1)} %get-tuple-element.181, f32[256,4352]{1,0:T(8,128)} %copy-done.2, f32[256]{0:T(256)S(1)} %fusion.42, f32[256]{0:T(256)S(1)} %get-tuple-element.156, bf16[8,512,128]{2,1,0:T(8,128)(2,1)} %get-tuple-element.182, s32[]{:T(128)} %get-tuple-element.166), kind=kOutput, calls=%fused_computation.12.clone.1 | convolution fusion | flops 1177911296 | bytes 9112064 | tf_op jit(solution)/shard_map/while/body/eval_jaxpr/dot_general | solution.py:62
  192.0 1.1 convolution_convert_fusion.3
  193.1 4.9 %fusion.41 = (f32[256]{0:T(256)S(1)}, f32[256,4352]{1,0:T(8,128)S(1)}) fusion(pred[256,4352]{1,0:T(32,128)(4,1)} %get-tuple-element.180, bf16[4352,576]{1,0:T(8,128)(2,1)} %get-tuple-element.179, bf16[256,64]{1,0:T(8,128)(2,1)S(1)} %slice.54, bf16[256,512]{1,0:T(8,128)(2,1)S(1)} %convolution_convert_fusion.3), kind=kOutput, calls=%fused_computation.63.clone.1 | convolution fusion | flops 1287388928 | bytes 10880000 | tf_op jit(solution)/shard_map/while/body/eval_jaxpr/dot_general | solution.py:49
  198.1 2.1 copy-done.2
  200.2 0.7 fusion.42
  201.0 5.1 %fusion.43 = bf16[1,256,128]{2,1,0:T(8,128)(2,1)S(1)} fusion(bf16[4352,512]{1,0:T(8,128)(2,1)} %get-tuple-element.181, f32[256,4352]{1,0:T(8,128)} %copy-done.2, f32[256]{0:T(256)S(1)} %fusion.42, f32[256]{0:T(256)S(1)} %get-tuple-element.156, bf16[8,512,128]{2,1,0:T(8,128)(2,1)} %get-tuple-element.182, s32[]{:T(128)} %get-tuple-element.166), kind=kOutput, calls=%fused_computation.12.clone.1 | convolution fusion | flops 1177911296 | bytes 9112064 | tf_op jit(solution)/shard_map/while/body/eval_jaxpr/dot_general | solution.py:62
  206.4 1.1 convolution_convert_fusion.3
  207.5 4.9 %fusion.41 = (f32[256]{0:T(256)S(1)}, f32[256,4352]{1,0:T(8,128)S(1)}) fusion(pred[256,4352]{1,0:T(32,128)(4,1)} %get-tuple-element.180, bf16[4352,576]{1,0:T(8,128)(2,1)} %get-tuple-element.179, bf16[256,64]{1,0:T(8,128)(2,1)S(1)} %slice.54, bf16[256,512]{1,0:T(8,128)(2,1)S(1)} %convolution_convert_fusion.3), kind=kOutput, calls=%fused_computation.63.clone.1 | convolution fusion | flops 1287388928 | bytes 10880000 | tf_op jit(solution)/shard_map/while/body/eval_jaxpr/dot_general | solution.py:49
  212.5 2.1 copy-done.2
  214.6 0.7 fusion.42
  215.3 5.1 %fusion.43 = bf16[1,256,128]{2,1,0:T(8,128)(2,1)S(1)} fusion(bf16[4352,512]{1,0:T(8,128)(2,1)} %get-tuple-element.181, f32[256,4352]{1,0:T(8,128)} %copy-done.2, f32[256]{0:T(256)S(1)} %fusion.42, f32[256]{0:T(256)S(1)} %get-tuple-element.156, bf16[8,512,128]{2,1,0:T(8,128)(2,1)} %get-tuple-element.182, s32[]{:T(128)} %get-tuple-element.166), kind=kOutput, calls=%fused_computation.12.clone.1 | convolution fusion | flops 1177911296 | bytes 9112064 | tf_op jit(solution)/shard_map/while/body/eval_jaxpr/dot_general | solution.py:62
  220.8 1.1 convolution_convert_fusion.3
  221.9 4.9 %fusion.41 = (f32[256]{0:T(256)S(1)}, f32[256,4352]{1,0:T(8,128)S(1)}) fusion(pred[256,4352]{1,0:T(32,128)(4,1)} %get-tuple-element.180, bf16[4352,576]{1,0:T(8,128)(2,1)} %get-tuple-element.179, bf16[256,64]{1,0:T(8,128)(2,1)S(1)} %slice.54, bf16[256,512]{1,0:T(8,128)(2,1)S(1)} %convolution_convert_fusion.3), kind=kOutput, calls=%fused_computation.63.clone.1 | convolution fusion | flops 1287388928 | bytes 10880000 | tf_op jit(solution)/shard_map/while/body/eval_jaxpr/dot_general | solution.py:49
  226.8 2.1 copy-done.2
  229.0 0.7 fusion.42
  229.7 5.1 %fusion.43 = bf16[1,256,128]{2,1,0:T(8,128)(2,1)S(1)} fusion(bf16[4352,512]{1,0:T(8,128)(2,1)} %get-tuple-element.181, f32[256,4352]{1,0:T(8,128)} %copy-done.2, f32[256]{0:T(256)S(1)} %fusion.42, f32[256]{0:T(256)S(1)} %get-tuple-element.156, bf16[8,512,128]{2,1,0:T(8,128)(2,1)} %get-tuple-element.182, s32[]{:T(128)} %get-tuple-element.166), kind=kOutput, calls=%fused_computation.12.clone.1 | convolution fusion | flops 1177911296 | bytes 9112064 | tf_op jit(solution)/shard_map/while/body/eval_jaxpr/dot_general | solution.py:62
  235.0 11.0 %convolution_convert_fusion.1 = bf16[256,7168]{1,0:T(8,128)(2,1)} fusion(bf16[256,1024]{0,1:T(8,128)(2,1)S(1)} %bitcast.66, bf16[1024,7168]{1,0:T(8,128)(2,1)} %param.19), kind=kOutput, calls=%fused_computation.26 | convolution fusion | flops 3759931392 | bytes 18874368 | tf_op jit(solution)/shard_map/dot_general | solution.py:102
  246.0 5.9 %copy.34 = bf16[256,7168]{0,1:T(8,128)(2,1)} copy(bf16[256,7168]{1,0:T(8,128)(2,1)} %convolution_convert_fusion.1) | data formatting | bytes 7340032
  252.0 33.4 %reduce-scatter.4.cloned.1.call-done = bf16[896,256]{1,0:T(8,128)(2,1)} async-done(((bf16[7168,256]{1,0:T(8,128)(2,1)}), bf16[896,256]{1,0:T(8,128)(2,1)}) %reduce-scatter.4.cloned.1.call-update) | async-done | bytes 458768
  285.4 2.0 copy.35
  (83 shorter events, 3.4 us)
Async XLA Ops:
  6.5 2.4 copy-start
  10.7 27.9 %all-to-all-start = ((bf16[16,4,16,576]{3,2,1,0:T(8,128)(2,1)}), bf16[16,4,16,576]{3,2,1,0:T(8,128)(2,1)S(1)}, u32[]{:S(2)}, u32[]{:S(2)}) async-start(bf16[16,4,16,576]{3,2,1,0:T(8,128)(2,1)} %bitcast.7), calls=%async_computation | async-start | bytes 2621440 | tf_op jit(solution)/shard_map/all_to_all | solution.py:87
  42.1 5.5 %copy-start.5 = (bf16[256,576]{0,1:T(8,128)(2,1)S(1)}, bf16[256,576]{0,1:T(8,128)(2,1)}, u32[]{:S(2)}) copy-start(bf16[256,576]{0,1:T(8,128)(2,1)} %param.12) | copy-start | bytes 884740
  42.1 5.7 %copy-start.6 = (s32[1,2,32]{2,1,0:T(2,128)S(1)}, s32[1,2,32]{2,1,0:T(2,128)}, u32[]{:S(2)}) copy-start(s32[1,2,32]{2,1,0:T(2,128)} %param.16) | copy-start | bytes 772
  42.1 8.6 %copy-start.3 = (bf16[256,1536]{1,0:T(8,128)(2,1)S(1)}, bf16[256,1536]{1,0:T(8,128)(2,1)}, u32[]{:S(2)}) copy-start(bf16[256,1536]{1,0:T(8,128)(2,1)} %param.11) | copy-start | bytes 2359300
  42.1 66.4 %all-to-all-start.1 = ((bf16[8,32,16,576]{3,2,1,0:T(8,128)(2,1)}), bf16[8,32,16,576]{3,2,1,0:T(8,128)(2,1)}, u32[]{:S(2)}, u32[]{:S(2)}) async-start(bf16[8,32,16,576]{3,2,1,0:T(8,128)(2,1)} %stack.2), calls=%async_computation.1 | async-start | bytes 10485760 | tf_op jit(solution)/shard_map/all_to_all | solution.py:90
  47.5 3.5 %copy-start.7 = (s32[1,32]{1,0:T(1,128)S(1)}, s32[1,32]{1,0:T(1,128)}, u32[]{:S(2)}) copy-start(s32[1,32]{1,0:T(1,128)} %param.15) | copy-start | bytes 388
  47.5 237.8 %reduce-scatter.4.cloned.1.call-start = ((), (), s32[]{:S(2)}) async-start(), calls=%async_computation.3 | async-start | bytes 4128768
  117.5 2.5 copy-start.4
  126.2 2.1 copy-start.2
  140.5 2.1 copy-start.2
  154.9 2.1 copy-start.2
  169.3 2.1 copy-start.2
  183.7 2.1 copy-start.2
  198.1 2.1 copy-start.2
  212.5 2.1 copy-start.2
  226.8 2.1 copy-start.2
  235.0 52.3 %copy-start.1 = (bf16[32,16,576]{2,1,0:T(8,128)(2,1)S(1)}, bf16[32,16,576]{2,1,0:T(8,128)(2,1)}, u32[]{:S(2)}) copy-start(bf16[32,16,576]{2,1,0:T(8,128)(2,1)} %param.13) | copy-start | bytes 1769476
Sparse Core Ops, SparseCore 0:
  252.1 33.2 reduce-scatter.3
